TPU v7x, 32 devices: a whole 2x2x4 slice. The times are simulated.
32 devices in a mesh: groups: 2 (over y), dom: 4 (over z), shot: 4 (over x, core).
Axes of the slice: x: 2, y: 2, z: 4, core: 2. Of those that a mesh axis runs over, the one named last changes fastest.
Arguments:
- courant_sq: float32 [128, 128, 128], P(('groups', 'dom')), parts along dimension 0, may hold values from 0.05 to 0.19
- adjoint_init: float32 [8, 2, 64, 128, 128], P(('groups', 'shot'), None, 'dom'), parts along dimension 0, may hold values from -6 to 6
- forward_saved: bfloat16 [8, 6, 64, 128, 128], P(('groups', 'shot'), None, 'dom'), parts along dimension 0, may hold values from -4 to 4
- residual_traces: float32 [8, 4, 1024], P(('groups', 'shot')), parts along dimension 0, may hold values from -6 to 6
- receivers: int32 [8, 1024, 3], P(('groups', 'shot')), parts along dimension 0, may hold values from 0 to 127, as said below
- sources: int32 [8, 3], P(('groups', 'shot')), parts along dimension 0, may hold values from 0 to 127, as said below
Outputs:
- gradient: float32 [128, 128, 128], P(('groups', 'dom'), 'shot'), parts along dimension 0
- adjoint_final: float32 [8, 2, 64, 128, 128], P(('groups', 'shot'), None, 'dom'), parts along dimension 0
There are 2 independent parts, one for each index of `groups`. A program takes and returns all parts, laid end to end along the dimension named above; each array names one. Nothing has to cross between parts.
Inputs may be any that keep to these rules, and one draw needn't show every extreme that they name: Each row holds the depth index (below 64), the first horizontal index (below 128) and the second (below 128) of a cell; receivers may share cells. `sources`: each row holds the depth index (below 64), the first horizontal index (below 128) and the second (below 128) of a cell.
All inputs are finite; a program needn't handle non-finite values.
Results may differ from a plain program's by a relative error of at most 0.0003.
Values sent between devices are 32-bit elements; how exact they have to be, the bound alone decides.
A program may use at most 64 MiB of HBM per device.

v0:
```python
import jax
import jax.numpy as jnp
from jax import lax
from jax.sharding import PartitionSpec as P

ITERS = 4
RADIUS = 6


STENCIL_WEIGHTS = (-205.0 / 72.0, 8.0 / 5.0, -1.0 / 5.0, 8.0 / 315.0, -1.0 / 560.0)


def padded_2(array, sides, width):
    for axis, dim in sides:
        size, length = (lax.axis_size(axis), array.shape[dim])
        up = [(i, (i + 1) % size) for i in range(size - 1)]
        down = [(j, i) for i, j in up]
        last = lax.slice_in_dim(array, length - width, length, axis=dim)
        initial = lax.slice_in_dim(array, 0, width, axis=dim)
        before = lax.ppermute(last, axis, up)
        after = lax.ppermute(initial, axis, down)
        array = jnp.concatenate([before, array, after], axis=dim)
    return array


def stencil(level_now):
    row_count = level_now.shape[0] - 8
    size_x = level_now.shape[1]
    size_y = level_now.shape[2]
    center = level_now[4 : 4 + row_count]
    padded = jnp.pad(center, ((0, 0), (4, 4), (4, 4)))
    summed = 3.0 * STENCIL_WEIGHTS[0] * center
    for offset in range(1, 5):
        beside_all = (
            level_now[4 + offset : 4 + offset + row_count]
            + level_now[4 - offset : 4 - offset + row_count]
        )
        beside_all = beside_all + padded[:, 4 + offset : 4 + offset + size_x, 4 : 4 + size_y]
        beside_all = beside_all + padded[:, 4 - offset : 4 - offset + size_x, 4 : 4 + size_y]
        beside_all = beside_all + padded[:, 4 : 4 + size_x, 4 + offset : 4 + offset + size_y]
        beside_all = beside_all + padded[:, 4 : 4 + size_x, 4 - offset : 4 - offset + size_y]
        summed = summed + STENCIL_WEIGHTS[offset] * beside_all
    return summed


def source_taper(source, depth_first, size_z, size_x, size_y):
    depth_gap = jnp.arange(size_z, dtype=jnp.int32) + depth_first - source[0]
    across_gap = jnp.arange(size_x, dtype=jnp.int32) - source[1]
    along_gap = jnp.arange(size_y, dtype=jnp.int32) - source[2]
    distance = (
        (depth_gap * depth_gap)[:, None, None]
        + (across_gap * across_gap)[None, :, None]
        + (along_gap * along_gap)[None, None, :]
    )
    return 1.0 - jnp.exp(-distance.astype(jnp.float32) / float(RADIUS * RADIUS))


def advance(
    level_later,
    level_now,
    courant_ext,
    first_row,
    section_top,
    forward_saved,
    residual_traces,
    receivers,
    summed,
):
    slab_rows = forward_saved.shape[2]
    row_count = level_now.shape[0] - 8
    margin_out = (row_count - slab_rows) // 2
    level_next = (
        2.0 * level_now[4 : 4 + row_count]
        - level_later[4 : 4 + row_count]
        + courant_ext * stencil(level_now)
    )
    top_row = first_row - margin_out
    local_rows = receivers[0, :, 0] - top_row
    inside = (local_rows >= 0) & (local_rows < row_count)
    amounts = jnp.where(inside, residual_traces[0, section_top], 0.0)
    level_next = level_next.at[
        jnp.clip(local_rows, 0, row_count - 1), receivers[0, :, 1], receivers[0, :, 2]
    ].add(amounts)
    forward_accel = (
        forward_saved[0, section_top + 2].astype(jnp.float32)
        - 2.0 * forward_saved[0, section_top + 1].astype(jnp.float32)
        + forward_saved[0, section_top].astype(jnp.float32)
    )
    summed = summed + level_next * forward_accel
    level_later = level_now[4 : 4 + row_count]
    return (level_later, level_next, summed)


def per_device(courant_sq, adjoint_init, forward_saved, residual_traces, receivers, sources):
    slab_rows, size_x, size_y = courant_sq.shape
    first_row = lax.axis_index("dom") * slab_rows
    level_later = adjoint_init[0, 0]
    level_now = adjoint_init[0, 1]
    summed = jnp.zeros((slab_rows, size_x, size_y), jnp.float32)
    for block_index in range(ITERS):
        padded_now = padded_2(level_now, (("dom", 0),), 4)
        padded_later = jnp.pad(level_later, ((4, 4), (0, 0), (0, 0)))
        level_later, level_now, summed = advance(
            padded_later,
            padded_now,
            courant_sq,
            first_row,
            ITERS - 1 - block_index,
            forward_saved,
            residual_traces,
            receivers,
            summed,
        )
    tapered = source_taper(sources[0], first_row, slab_rows, size_x, size_y) * summed
    gradient = lax.psum_scatter(tapered, "shot", scatter_dimension=1, tiled=True)
    return (gradient, jnp.stack([level_later, level_now])[None])


def solution(mesh):
    placed = (
        P(("groups", "dom"), None, None),
        P(("groups", "shot"), None, "dom", None, None),
        P(("groups", "shot"), None, "dom", None, None),
        P(("groups", "shot"), None, None),
        P(("groups", "shot"), None, None),
        P(("groups", "shot"), None),
    )
    return jax.shard_map(
        per_device,
        mesh=mesh,
        in_specs=placed,
        out_specs=(
            P(("groups", "dom"), "shot", None),
            P(("groups", "shot"), None, "dom", None, None),
        ),
        check_vma=False,
    )
```

profile of v0, /device:TPU:0, one launch (start us, length us, event | category | flops | bytes accessed | tf_op | source)
XLA Modules:
  0.0 136.1 jit_solution(18302973571200368317)
XLA Ops:
  7.2 0.0 reduce-scatter.2.cloned.1.call-start
  7.2 1.1 slice_bitcast_fusion.2
  8.3 0.0 copy-start.1
  8.3 5.1 %collective-permute-start.1 = (f32[4,128,128]{2,1,0:T(8,128)S(1)}, f32[4,128,128]{2,1,0:T(8,128)S(1)}, u32[]{:S(2)}, u32[]{:S(2)}) collective-permute-start(f32[4,128,128]{2,1,0:T(8,128)S(1)} %get-tuple-element.3), channel_id=1, source_target_pairs={{0,4},{4,8},{8,12},{1,5},{5,9},{9,13},{2,6},{6,10},{10,14},{3,7},{... | collective-permute-start | bytes 786440 | tf_op jit(solution)/shard_map/ppermute | solution.py:20
  13.4 1.3 collective-permute-start
  14.7 0.7 compare_select_fusion.2
  15.5 0.7 and_reduce_fusion.1
  16.2 0.7 and_reduce_fusion
  16.9 0.7 multiply_reduce_fusion
  17.7 0.9 fusion.157
  18.6 1.3 slice_bitcast_fusion
  19.9 0.0 collective-permute-done.1
  19.9 3.3 %collective-permute-done = f32[4,128,128]{2,1,0:T(8,128)} collective-permute-done((f32[4,128,128]{2,1,0:T(8,128)S(1)}, f32[4,128,128]{2,1,0:T(8,128)}, u32[]{:S(2)}, u32[]{:S(2)}) %collective-permute-start) | collective-permute-done | bytes 262176 | tf_op jit(solution)/shard_map/ppermute | solution.py:21
  23.2 0.0 copy-done.1
  23.2 4.6 %fusion.105 = f32[16,128,128]{2,1,0:T(8,128)S(1)} fusion(f32[16,128,128]{2,1,0:T(8,128)S(1)} %copy-done.1, f32[16,128,128]{2,1,0:T(8,128)S(1)} %slice_bitcast_fusion, f32[4,128,128]{2,1,0:T(8,128)S(1)} %collective-permute-done.1, f32[4,128,128]{2,1,0:T(8,128)} %collective-permute-done, f32[1,2,16,128,128]{4,3,2,1,0:T(8,128)} %param.7), kind=kLoop, calls=%fused_computation.232 | loop fusion | flops 10747904 | bytes 4718592 | tf_op jit(solution)/shard_map/add | solution.py:73
  27.8 6.5 %scatter_fusion = f32[262144]{0:T(1024)S(1)} fusion(f32[262144]{0:T(1024)S(1)} %bitcast.61, s32[1024]{0:T(1024)S(1)} %broadcast_select_fusion, f32[1024]{0:T(1024)S(1)} %get-tuple-element.20), kind=kCustom, calls=%fused_computation | custom fusion | flops 1024 | bytes 16384
  34.3 3.5 %collective-permute-start.3 = (f32[4,128,128]{2,1,0:T(8,128)S(1)}, f32[4,128,128]{2,1,0:T(8,128)S(1)}, u32[]{:S(2)}, u32[]{:S(2)}) collective-permute-start(f32[4,128,128]{2,1,0:T(8,128)S(1)} %bitcast.81), channel_id=1, source_target_pairs={{0,4},{4,8},{8,12},{1,5},{5,9},{9,13},{2,6},{6,10},{10,14},{3,7},{... | collective-permute-start | bytes 786440 | tf_op jit(solution)/shard_map/ppermute | solution.py:20
  37.8 1.3 collective-permute-start.2
  39.1 3.1 %collective-permute-done.3 = f32[4,128,128]{2,1,0:T(8,128)S(1)} collective-permute-done((f32[4,128,128]{2,1,0:T(8,128)S(1)}, f32[4,128,128]{2,1,0:T(8,128)S(1)}, u32[]{:S(2)}, u32[]{:S(2)}) %collective-permute-start.3) | collective-permute-done | bytes 262176 | tf_op jit(solution)/shard_map/ppermute | solution.py:20
  42.2 4.1 %collective-permute-done.2 = f32[4,128,128]{2,1,0:T(8,128)S(1)} collective-permute-done((f32[4,128,128]{2,1,0:T(8,128)S(1)}, f32[4,128,128]{2,1,0:T(8,128)S(1)}, u32[]{:S(2)}, u32[]{:S(2)}) %collective-permute-start.2) | collective-permute-done | bytes 262176 | tf_op jit(solution)/shard_map/ppermute | solution.py:21
  46.3 4.7 %fusion.75 = f32[16,128,128]{2,1,0:T(8,128)S(1)} fusion(f32[16,128,128]{2,1,0:T(8,128)S(1)} %copy-done.1, f32[16,128,128]{2,1,0:T(8,128)S(1)} %bitcast.62, f32[4,128,128]{2,1,0:T(8,128)S(1)} %collective-permute-done.3, f32[4,128,128]{2,1,0:T(8,128)S(1)} %collective-permute-done.2, f32[1,2,16,128,128]{4,3,2,1,0:T(8,128)} %param.7), kind=kLoop, calls=%fused_computation.202 | loop fusion | flops 10747904 | bytes 4718592 | tf_op jit(solution)/shard_map/add | solution.py:73
  51.0 0.0 copy-start.4
  51.0 6.5 %scatter_fusion.1 = f32[262144]{0:T(1024)S(1)} fusion(f32[262144]{0:T(1024)S(1)} %bitcast.65, s32[1024]{0:T(1024)S(1)} %broadcast_select_fusion, f32[1024]{0:T(1024)S(1)} %get-tuple-element.19), kind=kCustom, calls=%fused_computation.1 | custom fusion | flops 1024 | bytes 16384
  57.5 0.0 copy-start.2
  57.5 3.6 %collective-permute-start.5 = (f32[4,128,128]{2,1,0:T(8,128)S(1)}, f32[4,128,128]{2,1,0:T(8,128)S(1)}, u32[]{:S(2)}, u32[]{:S(2)}) collective-permute-start(f32[4,128,128]{2,1,0:T(8,128)S(1)} %bitcast.78), channel_id=1, source_target_pairs={{0,4},{4,8},{8,12},{1,5},{5,9},{9,13},{2,6},{6,10},{10,14},{3,7},{... | collective-permute-start | bytes 786440 | tf_op jit(solution)/shard_map/ppermute | solution.py:20
  61.2 1.3 collective-permute-start.4
  62.5 0.0 copy-done.4
  62.5 0.6 fusion.158
  63.1 0.6 subtract_multiply_fusion
  63.7 0.6 subtract_multiply_fusion.1
  64.3 0.7 collective-permute-done.5
  65.0 4.4 %collective-permute-done.4 = f32[4,128,128]{2,1,0:T(8,128)S(1)} collective-permute-done((f32[4,128,128]{2,1,0:T(8,128)S(1)}, f32[4,128,128]{2,1,0:T(8,128)S(1)}, u32[]{:S(2)}, u32[]{:S(2)}) %collective-permute-start.4) | collective-permute-done | bytes 262176 | tf_op jit(solution)/shard_map/ppermute | solution.py:21
  69.4 0.0 copy-done.2
  69.4 3.6 %fusion.45 = f32[16,128,128]{2,1,0:T(8,128)S(1)} fusion(f32[16,128,128]{2,1,0:T(8,128)S(1)} %copy-done.2, f32[16,128,128]{2,1,0:T(8,128)S(1)} %bitcast.66, f32[4,128,128]{2,1,0:T(8,128)S(1)} %collective-permute-done.5, f32[4,128,128]{2,1,0:T(8,128)S(1)} %collective-permute-done.4, f32[16,128,128]{2,1,0:T(8,128)S(1)} %bitcast.63), kind=kLoop, calls=%fused_computation.172 | loop fusion | flops 10747904 | bytes 4718592 | tf_op jit(solution)/shard_map/add | solution.py:73
  73.1 6.5 %scatter_fusion.2 = f32[262144]{0:T(1024)S(1)} fusion(f32[262144]{0:T(1024)S(1)} %bitcast.69, s32[1024]{0:T(1024)S(1)} %broadcast_select_fusion, f32[1024]{0:T(1024)S(1)} %get-tuple-element.18), kind=kCustom, calls=%fused_computation.2 | custom fusion | flops 1024 | bytes 16384
  79.5 0.0 copy-start.3
  79.6 2.7 %collective-permute-start.7 = (f32[4,128,128]{2,1,0:T(8,128)S(1)}, f32[4,128,128]{2,1,0:T(8,128)S(1)}, u32[]{:S(2)}, u32[]{:S(2)}) collective-permute-start(f32[4,128,128]{2,1,0:T(8,128)S(1)} %bitcast.79), channel_id=1, source_target_pairs={{0,4},{4,8},{8,12},{1,5},{5,9},{9,13},{2,6},{6,10},{10,14},{3,7},{... | collective-permute-start | bytes 786440 | tf_op jit(solution)/shard_map/ppermute | solution.py:20
  82.3 1.5 %collective-permute-start.6 = (f32[4,128,128]{2,1,0:T(8,128)S(1)}, f32[4,128,128]{2,1,0:T(8,128)S(1)}, u32[]{:S(2)}, u32[]{:S(2)}) collective-permute-start(f32[4,128,128]{2,1,0:T(8,128)S(1)} %bitcast.77), channel_id=1, source_target_pairs={{4,0},{8,4},{12,8},{5,1},{9,5},{13,9},{6,2},{10,6},{14,10},{7,3},{... | collective-permute-start | bytes 786440 | tf_op jit(solution)/shard_map/ppermute | solution.py:21
  83.8 0.7 subtract_multiply_fusion.2
  84.5 0.1 broadcast_add_fusion
  84.5 1.6 %collective-permute-done.7 = f32[4,128,128]{2,1,0:T(8,128)S(1)} collective-permute-done((f32[4,128,128]{2,1,0:T(8,128)S(1)}, f32[4,128,128]{2,1,0:T(8,128)S(1)}, u32[]{:S(2)}, u32[]{:S(2)}) %collective-permute-start.7) | collective-permute-done | bytes 262176 | tf_op jit(solution)/shard_map/ppermute | solution.py:20
  86.2 4.4 %collective-permute-done.6 = f32[4,128,128]{2,1,0:T(8,128)S(1)} collective-permute-done((f32[4,128,128]{2,1,0:T(8,128)S(1)}, f32[4,128,128]{2,1,0:T(8,128)S(1)}, u32[]{:S(2)}, u32[]{:S(2)}) %collective-permute-start.6) | collective-permute-done | bytes 262176 | tf_op jit(solution)/shard_map/ppermute | solution.py:21
  90.6 0.0 copy-done.3
  90.6 4.4 %fusion.15 = f32[16,128,128]{2,1,0:T(8,128)} fusion(f32[16,128,128]{2,1,0:T(8,128)S(1)} %copy-done.3, f32[16,128,128]{2,1,0:T(8,128)S(1)} %bitcast.70, f32[4,128,128]{2,1,0:T(8,128)S(1)} %collective-permute-done.7, f32[4,128,128]{2,1,0:T(8,128)S(1)} %collective-permute-done.6, f32[16,128,128]{2,1,0:T(8,128)S(1)} %bitcast.67), kind=kLoop, calls=%fused_computation.142 | loop fusion | flops 10747904 | bytes 4718592 | tf_op jit(solution)/shard_map/add | solution.py:73
  95.0 7.6 %scatter_fusion.3 = f32[262144]{0:T(1024)} fusion(f32[262144]{0:T(1024)} %bitcast.73, s32[1024]{0:T(1024)S(1)} %broadcast_select_fusion, f32[1024]{0:T(1024)S(1)} %get-tuple-element.17), kind=kCustom, calls=%fused_computation.3 | custom fusion | flops 1024 | bytes 16384
  102.6 3.5 %fusion.4 = f32[16,128,128]{2,1,0:T(8,128)} fusion(f32[16,128,128]{2,1,0:T(8,128)S(1)} %bitcast.71, f32[16,128,128]{2,1,0:T(8,128)S(1)} %bitcast.64, f32[16,128,128]{2,1,0:T(8,128)S(1)} %bitcast.68, f32[16,128,128]{2,1,0:T(8,128)} %bitcast.74, bf16[1,6,16,128,128]{4,3,2,1,0:T(8,128)(2,1)} %param.8, s32[128]{0:T(128)S(1)} %subtract_multiply_fusion, ...), kind=kLoop, calls=%fused_computation.131 | loop fusion | flops 8126464 | bytes 8397312 | tf_op jit(solution)/shard_map/mul | solution.py:114
  106.1 0.0 copy-start
  106.1 0.0 reduce-scatter.2.cloned.1.call-update
  106.2 1.2 copy-done
  107.4 1.5 %maximum_bitcast_fusion = f32[1,2,16,128,128]{4,3,2,1,0:T(8,128)} fusion(f32[1,16,128,128]{3,2,1,0:T(8,128)S(1)} %bitcast.75, f32[1,16,128,128]{3,2,1,0:T(8,128)S(1)} %bitcast.72), kind=kLoop, calls=%fused_computation.92 | loop fusion | flops 524288 | bytes 4194304 | tf_op jit(solution)/shard_map/broadcast_in_dim | solution.py:116
  108.8 20.5 %reduce-scatter.2.cloned.1.call-done = f32[16,32,128]{2,1,0:T(8,128)} async-done(((f32[16,128,128]{2,1,0:T(8,128)}), f32[16,32,128]{2,1,0:T(8,128)}) %reduce-scatter.2.cloned.1.call-update) | async-done | bytes 262160 | tf_op jit(solution)/shard_map/reduce_scatter | solution.py:115
  (5 shorter events, 0.1 us)
Async XLA Ops:
  7.2 122.1 %reduce-scatter.2.cloned.1.call-start = ((), (), s32[]{:S(2)}) async-start(), calls=%async_computation.1 | async-start | bytes 1310720 | tf_op jit(solution)/shard_map/reduce_scatter | solution.py:115
  8.3 14.9 %copy-start.1 = (f32[16,128,128]{2,1,0:T(8,128)S(1)}, f32[16,128,128]{2,1,0:T(8,128)}, u32[]{:S(2)}) copy-start(f32[16,128,128]{2,1,0:T(8,128)} %param.6) | copy-start | bytes 3145732
  8.3 11.6 %collective-permute-start.1 = (f32[4,128,128]{2,1,0:T(8,128)S(1)}, f32[4,128,128]{2,1,0:T(8,128)S(1)}, u32[]{:S(2)}, u32[]{:S(2)}) collective-permute-start(f32[4,128,128]{2,1,0:T(8,128)S(1)} %get-tuple-element.3), channel_id=1, source_target_pairs={{0,4},{4,8},{8,12},{1,5},{5,9},{9,13},{2,6},{6,10},{10,14},{3,7},{... | collective-permute-start | bytes 786440 | tf_op jit(solution)/shard_map/ppermute | solution.py:20
  13.4 9.8 %collective-permute-start = (f32[4,128,128]{2,1,0:T(8,128)S(1)}, f32[4,128,128]{2,1,0:T(8,128)}, u32[]{:S(2)}, u32[]{:S(2)}) collective-permute-start(f32[4,128,128]{2,1,0:T(8,128)S(1)} %get-tuple-element.2), channel_id=1, source_target_pairs={{4,0},{8,4},{12,8},{5,1},{9,5},{13,9},{6,2},{10,6},{14,10},{7,3},{... | collective-permute-start | bytes 786440 | tf_op jit(solution)/shard_map/ppermute | solution.py:21
  34.3 7.9 %collective-permute-start.3 = (f32[4,128,128]{2,1,0:T(8,128)S(1)}, f32[4,128,128]{2,1,0:T(8,128)S(1)}, u32[]{:S(2)}, u32[]{:S(2)}) collective-permute-start(f32[4,128,128]{2,1,0:T(8,128)S(1)} %bitcast.81), channel_id=1, source_target_pairs={{0,4},{4,8},{8,12},{1,5},{5,9},{9,13},{2,6},{6,10},{10,14},{3,7},{... | collective-permute-start | bytes 786440 | tf_op jit(solution)/shard_map/ppermute | solution.py:20
  37.8 8.5 %collective-permute-start.2 = (f32[4,128,128]{2,1,0:T(8,128)S(1)}, f32[4,128,128]{2,1,0:T(8,128)S(1)}, u32[]{:S(2)}, u32[]{:S(2)}) collective-permute-start(f32[4,128,128]{2,1,0:T(8,128)S(1)} %bitcast.80), channel_id=1, source_target_pairs={{4,0},{8,4},{12,8},{5,1},{9,5},{13,9},{6,2},{10,6},{14,10},{7,3},{... | collective-permute-start | bytes 786440 | tf_op jit(solution)/shard_map/ppermute | solution.py:21
  51.0 11.5 %copy-start.4 = (s32[1,3]{1,0:T(1,128)S(1)}, s32[1,3]{1,0:T(1,128)}, u32[]{:S(2)}) copy-start(s32[1,3]{1,0:T(1,128)} %param.11) | copy-start | bytes 40
  57.5 11.9 %copy-start.2 = (f32[16,128,128]{2,1,0:T(8,128)S(1)}, f32[16,128,128]{2,1,0:T(8,128)}, u32[]{:S(2)}) copy-start(f32[16,128,128]{2,1,0:T(8,128)} %param.6) | copy-start | bytes 3145732
  57.5 7.5 %collective-permute-start.5 = (f32[4,128,128]{2,1,0:T(8,128)S(1)}, f32[4,128,128]{2,1,0:T(8,128)S(1)}, u32[]{:S(2)}, u32[]{:S(2)}) collective-permute-start(f32[4,128,128]{2,1,0:T(8,128)S(1)} %bitcast.78), channel_id=1, source_target_pairs={{0,4},{4,8},{8,12},{1,5},{5,9},{9,13},{2,6},{6,10},{10,14},{3,7},{... | collective-permute-start | bytes 786440 | tf_op jit(solution)/shard_map/ppermute | solution.py:20
  61.2 8.3 %collective-permute-start.4 = (f32[4,128,128]{2,1,0:T(8,128)S(1)}, f32[4,128,128]{2,1,0:T(8,128)S(1)}, u32[]{:S(2)}, u32[]{:S(2)}) collective-permute-start(f32[4,128,128]{2,1,0:T(8,128)S(1)} %bitcast.76), channel_id=1, source_target_pairs={{4,0},{8,4},{12,8},{5,1},{9,5},{13,9},{6,2},{10,6},{14,10},{7,3},{... | collective-permute-start | bytes 786440 | tf_op jit(solution)/shard_map/ppermute | solution.py:21
  79.5 11.0 %copy-start.3 = (f32[16,128,128]{2,1,0:T(8,128)S(1)}, f32[16,128,128]{2,1,0:T(8,128)}, u32[]{:S(2)}) copy-start(f32[16,128,128]{2,1,0:T(8,128)} %param.6) | copy-start | bytes 3145732
  79.6 6.6 %collective-permute-start.7 = (f32[4,128,128]{2,1,0:T(8,128)S(1)}, f32[4,128,128]{2,1,0:T(8,128)S(1)}, u32[]{:S(2)}, u32[]{:S(2)}) collective-permute-start(f32[4,128,128]{2,1,0:T(8,128)S(1)} %bitcast.79), channel_id=1, source_target_pairs={{0,4},{4,8},{8,12},{1,5},{5,9},{9,13},{2,6},{6,10},{10,14},{3,7},{... | collective-permute-start | bytes 786440 | tf_op jit(solution)/shard_map/ppermute | solution.py:20
  82.3 8.3 %collective-permute-start.6 = (f32[4,128,128]{2,1,0:T(8,128)S(1)}, f32[4,128,128]{2,1,0:T(8,128)S(1)}, u32[]{:S(2)}, u32[]{:S(2)}) collective-permute-start(f32[4,128,128]{2,1,0:T(8,128)S(1)} %bitcast.77), channel_id=1, source_target_pairs={{4,0},{8,4},{12,8},{5,1},{9,5},{13,9},{6,2},{10,6},{14,10},{7,3},{... | collective-permute-start | bytes 786440 | tf_op jit(solution)/shard_map/ppermute | solution.py:21
  106.1 1.2 copy-start
Sparse Core Ops, SparseCore 0:
  106.3 22.9 reduce-scatter.1
where the time goes:
time: 137 us; the launch traced here: 136 us
  other arithmetic  54.2 us (40%)
  waiting for transfers between devices  42.2 us (31%)
  starting transfers between devices  20.3 us (15%)
  between operations  14.3 us (10%)
  local copies, waits for them, and re-layouts  5.17 us (4%)
    unnamed x7, other arithmetic  28.5 us
    reduce_scatter x1, waiting for transfers between devices, per_device(): lax.psum_scatter(tapered, 'shot', scatter_dimension=1, tiled=True)  20.5 us
    add x4, other arithmetic, advance(): 2.0 * level_now[4:4 + row_count] - level_later[4:4 + row_count]  17.3 us
    ppermute x4, waiting for transfers between devices, padded_2(): after = lax.ppermute(initial, axis, down)  16.2 us
    ppermute x4, starting transfers between devices, padded_2(): before = lax.ppermute(last, axis, up)  14.9 us
    ppermute x4, waiting for transfers between devices, padded_2(): before = lax.ppermute(last, axis, up)  5.48 us
    ppermute x4, starting transfers between devices, padded_2(): after = lax.ppermute(initial, axis, down)  5.35 us
    mul x1, other arithmetic, per_device(): source_taper(sources[0], first_row, slab_rows, size_x, size_y) * summed  3.52 us
  transfers between devices with their start and end apart: 9, of which 8 were waited for; matrix products, arithmetic and copies ran while one was open for 7% of the time, Pallas kernels for 0%

commit v1 on v0

v1 whole, which is shorter than its diff:
```python
import functools

import jax
import jax.numpy as jnp
from jax import lax
from jax.experimental import pallas as pl
from jax.experimental.pallas import tpu as pltpu
from jax.sharding import PartitionSpec as P

ITERS = 4
RADIUS = 6
HALO = 4
PAD = 8

STENCIL_WEIGHTS = (-205.0 / 72.0, 8.0 / 5.0, -1.0 / 5.0, 8.0 / 315.0, -1.0 / 560.0)


def kernel(
    dom_n,
    shot_n,
    source_ref,
    spot_ref,
    trace_ref,
    courant_hbm,
    init_hbm,
    fwd_hbm,
    grad_ref,
    final_hbm,
    lev,
    courant,
    fwd,
    image,
    hot,
    src,
    band,
    parts,
    in_sem,
    send_sem,
    recv_sem,
    part_send,
    part_recv,
    out_sem,
):
    slab, size_x, size_y = courant.shape
    rows = size_x // shot_n
    me = lax.axis_index("dom")
    shot = lax.axis_index("shot")
    has_up = me > 0
    has_down = me < dom_n - 1

    loads = [
        pltpu.make_async_copy(
            init_hbm.at[1], lev.at[1, pl.ds(HALO, slab), pl.ds(PAD, size_x), :], in_sem.at[0]
        ),
        pltpu.make_async_copy(
            init_hbm.at[0], lev.at[0, pl.ds(HALO, slab), pl.ds(PAD, size_x), :], in_sem.at[1]
        ),
        pltpu.make_async_copy(courant_hbm, courant, in_sem.at[2]),
        pltpu.make_async_copy(fwd_hbm, fwd, in_sem.at[3]),
    ]
    for load in loads:
        load.start()

    @pl.when(jnp.logical_not(has_up))
    def _():
        for level in range(1, ITERS + 1):
            lev[level, 0:HALO] = jnp.zeros((HALO, size_x + 2 * PAD, size_y), jnp.float32)

    @pl.when(jnp.logical_not(has_down))
    def _():
        for level in range(1, ITERS + 1):
            lev[level, HALO + slab :] = jnp.zeros((HALO, size_x + 2 * PAD, size_y), jnp.float32)

    barrier = pltpu.get_barrier_semaphore()

    @pl.when(has_up)
    def _():
        pl.semaphore_signal(barrier, inc=1, device_id={"dom": me - 1})

    @pl.when(has_down)
    def _():
        pl.semaphore_signal(barrier, inc=1, device_id={"dom": me + 1})

    for d in range(1, shot_n):
        pl.semaphore_signal(barrier, inc=1, device_id={"shot": lax.rem(shot + d, shot_n)})
    pl.semaphore_wait(
        barrier, has_up.astype(jnp.int32) + has_down.astype(jnp.int32) + (shot_n - 1)
    )

    def halo_copies(step, strip):
        level = step + 1
        cut = pl.ds(PAD + strip * rows, rows)
        if step == 0:
            plain = pl.ds(strip * rows, rows)
            low = init_hbm.at[1, pl.ds(0, HALO), plain, :]
            high = init_hbm.at[1, pl.ds(slab - HALO, HALO), plain, :]
        else:
            low = lev.at[level, pl.ds(HALO, HALO), cut, :]
            high = lev.at[level, pl.ds(slab, HALO), cut, :]
        upward = pltpu.make_async_remote_copy(
            src_ref=low,
            dst_ref=lev.at[level, pl.ds(HALO + slab, HALO), cut, :],
            send_sem=send_sem.at[step, 0, strip],
            recv_sem=recv_sem.at[step, 0, strip],
            device_id={"dom": me - 1},
        )
        downward = pltpu.make_async_remote_copy(
            src_ref=high,
            dst_ref=lev.at[level, pl.ds(0, HALO), cut, :],
            send_sem=send_sem.at[step, 1, strip],
            recv_sem=recv_sem.at[step, 1, strip],
            device_id={"dom": me + 1},
        )
        return upward, downward

    def send_halo(step, strip):
        upward, downward = halo_copies(step, strip)

        @pl.when(has_up)
        def _():
            upward.start()

        @pl.when(has_down)
        def _():
            downward.start()

    def wait_halo(step, strip):
        upward, downward = halo_copies(step, strip)

        @pl.when(has_down)
        def _():
            upward.wait_recv()

        @pl.when(has_up)
        def _():
            downward.wait_recv()

    def wait_sent(step, strip):
        upward, downward = halo_copies(step, strip)

        @pl.when(has_up)
        def _():
            upward.wait_send()

        @pl.when(has_down)
        def _():
            downward.wait_send()

    for strip in range(shot_n):
        send_halo(0, strip)

    for level in range(1, ITERS + 1):
        lev[level, HALO : HALO + slab, 0:PAD] = jnp.zeros((slab, PAD, size_y), jnp.float32)
        lev[level, HALO : HALO + slab, PAD + size_x :] = jnp.zeros(
            (slab, PAD, size_y), jnp.float32
        )
    gap = jnp.abs(
        lax.broadcasted_iota(jnp.int32, (size_y, size_y), 0)
        - lax.broadcasted_iota(jnp.int32, (size_y, size_y), 1)
    )
    weights = jnp.where(gap == 0, jnp.float32(3.0 * STENCIL_WEIGHTS[0]), jnp.float32(0.0))
    for offset in range(1, HALO + 1):
        weights = jnp.where(gap == offset, jnp.float32(STENCIL_WEIGHTS[offset]), weights)
    band[...] = weights

    n_rec = spot_ref.shape[1]

    @pl.loop(0, slab)
    def _(z):
        row = lax.broadcasted_iota(jnp.int32, (size_x, n_rec), 0) + z * size_x
        same = row == spot_ref[0:1, :]
        hot[pl.ds(pl.multiple_of(z * size_x, size_x), size_x), :] = jnp.where(
            same, 1.0, 0.0
        ).astype(jnp.bfloat16)

    def place(section):
        amount = trace_ref[section : section + 1, :]
        high = amount.astype(jnp.bfloat16).astype(jnp.float32)
        low = amount - high
        same = lax.broadcasted_iota(jnp.int32, (size_y, n_rec), 0) == spot_ref[1:2, :]
        columns = jnp.concatenate(
            [jnp.where(same, high, 0.0), jnp.where(same, low, 0.0)], axis=0
        ).astype(jnp.bfloat16)
        block = 4 * size_x

        @pl.loop(0, slab * size_x // block)
        def _(i):
            cut = pl.ds(pl.multiple_of(i * block, block), block)
            src[cut, :] = lax.dot_general(
                hot[cut, :],
                columns,
                (((1,), (1,)), ((), ())),
                preferred_element_type=jnp.float32,
            )

    def update(step, z, planes, first, count):
        level = step + 1
        section = ITERS - 1 - step
        cut = pl.ds(PAD + first, count)
        plain = pl.ds(first, count)
        here = pl.ds(z, planes)
        now = lev[level, pl.ds(HALO + z, planes), cut, :]
        total = lax.dot_general(
            now.reshape(planes * count, size_y),
            band[...],
            (((1,), (0,)), ((), ())),
            precision=lax.Precision.HIGHEST,
            preferred_element_type=jnp.float32,
        ).reshape(planes, count, size_y)
        for offset in range(1, HALO + 1):
            beside = (
                lev[level, pl.ds(HALO + z + offset, planes), cut, :]
                + lev[level, pl.ds(HALO + z - offset, planes), cut, :]
                + lev[level, pl.ds(HALO + z, planes), pl.ds(PAD + first + offset, count), :]
                + lev[level, pl.ds(HALO + z, planes), pl.ds(PAD + first - offset, count), :]
            )
            total = total + STENCIL_WEIGHTS[offset] * beside
        added = []
        for p in range(planes):
            at = pl.ds(pl.multiple_of((z + p) * size_x + first, 8), count)
            added.append(src[at, 0:size_y] + src[at, size_y : 2 * size_y])
        added = added[0][None] if planes == 1 else jnp.stack(added)
        later = lev[level - 1, pl.ds(HALO + z, planes), cut, :]
        new = 2.0 * now - later + courant[here, plain, :] * total + added
        lev[level + 1, pl.ds(HALO + z, planes), cut, :] = new
        accel = (
            fwd[section + 2, here, plain, :].astype(jnp.float32)
            - 2.0 * fwd[section + 1, here, plain, :].astype(jnp.float32)
            + fwd[section, here, plain, :].astype(jnp.float32)
        )
        value = new * accel
        if step > 0:
            value = value + image[here, plain, :]
        if step == ITERS - 1:
            shape = (planes, count, size_y)
            dz = lax.broadcasted_iota(jnp.int32, shape, 0) + (me * slab + z - source_ref[0])
            dx = lax.broadcasted_iota(jnp.int32, shape, 1) + (first - source_ref[1])
            dy = lax.broadcasted_iota(jnp.int32, shape, 2) - source_ref[2]
            distance = (dz * dz + dx * dx + dy * dy).astype(jnp.float32)
            value = value * (1.0 - jnp.exp(distance * (-1.0 / float(RADIUS * RADIUS))))
        image[here, plain, :] = value

    def part_copy(d, group, first_z, planes):
        target = lax.rem(shot + d, shot_n)
        return pltpu.make_async_remote_copy(
            src_ref=image.at[
                pl.ds(first_z, planes), pl.ds(pl.multiple_of(target * rows, 8), rows), :
            ],
            dst_ref=parts.at[d - 1, pl.ds(first_z, planes), :, :],
            send_sem=part_send.at[group, d - 1],
            recv_sem=part_recv.at[group, d - 1],
            device_id={"shot": target},
        )

    groups = ((HALO, slab - 2 * HALO), (0, HALO), (slab - HALO, HALO))

    def final_copy(index, group):
        first_z, planes = groups[group]
        return pltpu.make_async_copy(
            lev.at[ITERS + index, pl.ds(HALO + first_z, planes), pl.ds(PAD, size_x), :],
            final_hbm.at[index, pl.ds(first_z, planes)],
            out_sem.at[index, group],
        )

    for step in range(ITERS):
        last = step == ITERS - 1
        place(ITERS - 1 - step)
        if step == 0:
            for load in loads:
                load.wait()

        @pl.loop(HALO, slab - HALO)
        def _(z):
            update(step, z, 1, 0, size_x)

        if last:
            final_copy(1, 0).start()
            for d in range(1, shot_n):
                part_copy(d, 0, *groups[0]).start()

        for strip in range(shot_n):
            wait_halo(step, strip)
            update(step, 0, HALO, strip * rows, rows)
            update(step, slab - HALO, HALO, strip * rows, rows)
            if not last:
                send_halo(step + 1, strip)

        if step == ITERS - 2:
            for group in range(3):
                final_copy(0, group).start()

    for group in (1, 2):
        final_copy(1, group).start()
        for d in range(1, shot_n):
            part_copy(d, group, *groups[group]).start()

    for group in range(3):
        first_z, planes = groups[group]
        value = image[
            first_z : first_z + planes, pl.ds(pl.multiple_of(shot * rows, 8), rows), :
        ]
        for d in range(1, shot_n):
            part_copy(d, group, first_z, planes).wait_recv()
            value = value + parts[d - 1, first_z : first_z + planes]
        grad_ref[first_z : first_z + planes] = value

    for step in range(ITERS):
        for strip in range(shot_n):
            wait_sent(step, strip)
    for group in range(3):
        for d in range(1, shot_n):
            part_copy(d, group, *groups[group]).wait_send()
        final_copy(0, group).wait()
        final_copy(1, group).wait()


def per_device(
    dom_n, shot_n, courant_sq, adjoint_init, forward_saved, residual_traces, receivers, sources
):
    slab, size_x, size_y = courant_sq.shape
    n_rec = receivers.shape[1]
    first_row = lax.axis_index("dom") * slab
    spots = receivers[0]
    spot_rows = (spots[:, 0] - first_row) * size_x + spots[:, 1]
    spot = jnp.stack([spot_rows, spots[:, 2]])
    hbm = pl.BlockSpec(memory_space=pl.ANY)
    vmem = pl.BlockSpec(memory_space=pltpu.VMEM)
    gradient, final = pl.pallas_call(
        functools.partial(kernel, dom_n, shot_n),
        out_shape=(
            jax.ShapeDtypeStruct((slab, size_x // shot_n, size_y), jnp.float32),
            jax.ShapeDtypeStruct((2, slab, size_x, size_y), jnp.float32),
        ),
        in_specs=[pl.BlockSpec(memory_space=pltpu.SMEM), vmem, vmem, hbm, hbm, hbm],
        out_specs=(vmem, hbm),
        scratch_shapes=[
            pltpu.VMEM((ITERS + 2, slab + 2 * HALO, size_x + 2 * PAD, size_y), jnp.float32),
            pltpu.VMEM((slab, size_x, size_y), jnp.float32),
            pltpu.VMEM((ITERS + 2, slab, size_x, size_y), jnp.bfloat16),
            pltpu.VMEM((slab, size_x, size_y), jnp.float32),
            pltpu.VMEM((slab * size_x, n_rec), jnp.bfloat16),
            pltpu.VMEM((slab * size_x, 2 * size_y), jnp.float32),
            pltpu.VMEM((size_y, size_y), jnp.float32),
            pltpu.VMEM((shot_n - 1, slab, size_x // shot_n, size_y), jnp.float32),
            pltpu.SemaphoreType.DMA((4,)),
            pltpu.SemaphoreType.DMA((ITERS, 2, shot_n)),
            pltpu.SemaphoreType.DMA((ITERS, 2, shot_n)),
            pltpu.SemaphoreType.DMA((3, shot_n - 1)),
            pltpu.SemaphoreType.DMA((3, shot_n - 1)),
            pltpu.SemaphoreType.DMA((2, 3)),
        ],
        compiler_params=pltpu.CompilerParams(
            collective_id=0, has_side_effects=True, vmem_limit_bytes=60 * 1024 * 1024
        ),
    )(
        sources[0],
        spot,
        residual_traces[0],
        courant_sq,
        adjoint_init[0],
        forward_saved[0],
    )
    return gradient, final[None]


def solution(mesh):
    placed = (
        P(("groups", "dom"), None, None),
        P(("groups", "shot"), None, "dom", None, None),
        P(("groups", "shot"), None, "dom", None, None),
        P(("groups", "shot"), None, None),
        P(("groups", "shot"), None, None),
        P(("groups", "shot"), None),
    )
    return jax.shard_map(
        functools.partial(per_device, mesh.shape["dom"], mesh.shape["shot"]),
        mesh=mesh,
        in_specs=placed,
        out_specs=(
            P(("groups", "dom"), "shot", None),
            P(("groups", "shot"), None, "dom", None, None),
        ),
        check_vma=False,
    )
```

time: 137 us -> 47.6 us (0.35)
  other arithmetic: 54.2 us -> 0.62 us
  waiting for transfers between devices: 42.2 us -> 0 us
  Pallas kernels: 0 us -> 40.5 us
  starting transfers between devices: 20.3 us -> 0 us
  between operations: 14.3 us -> 0.65 us
    pallas_call x0 -> x1, Pallas kernels: none -> 40.5 us  [per_device(): pl.pallas_call(functools.partial(kernel, dom_n, shot_n), out_shape=(jax.S...]
    unnamed x7 -> x0, other arithmetic: 28.5 us -> none
    ppermute x8 -> x0, waiting for transfers between devices: 21.7 us -> none  [the longest x4 16.2 us: padded_2(): after = lax.ppermute(initial, axis, down)]
    reduce_scatter x1 -> x0, waiting for transfers between devices: 20.5 us -> none  [per_device(): lax.psum_scatter(tapered, 'shot', scatter_dimension=1, tiled=True)]
    ppermute x8 -> x0, starting transfers between devices: 20.3 us -> none  [the longest x4 14.9 us: padded_2(): before = lax.ppermute(last, axis, up)]
    add x5 -> x1, other arithmetic: 17.4 us -> 0.01 us  [per_device(): spot_rows = (spots[:, 0] - first_row) * size_x + spots[:, 1]]
    mul x4 -> x0, other arithmetic: 5.38 us -> none  [the longest x1 3.52 us: per_device(): source_taper(sources[0], first_row, slab_rows, size_x, size_y) * summed]
    unnamed x10 -> x3, local copies, waits for them, and re-layouts: 1.23 us -> 5.52 us
  transfers between devices with their start and end apart: 9 -> 0, of which waited for: 8 -> 0; matrix products, arithmetic and copies ran while one was open for 7% -> 0% of each run, Pallas kernels for 0% -> 0%
where the time goes in v1:
time: 47.6 us; the launch traced here: 47.3 us
  Pallas kernels  40.5 us (85%)
  local copies, waits for them, and re-layouts  5.52 us (12%)
  between operations  0.65 us (1%)
  other arithmetic  0.62 us (1%)
    pallas_call x1, Pallas kernels, per_device(): pl.pallas_call(functools.partial(kernel, dom_n, shot_n), out_shape=(jax.S...  40.5 us
    unnamed x3, local copies, waits for them, and re-layouts  5.52 us

profile of v1, /device:TPU:0, one launch (start us, length us, event | category | flops | bytes accessed | tf_op | source)
XLA Modules:
  0.0 47.3 jit_solution(14581651277357669114)
XLA Ops:
  0.6 0.7 %copy.10 = s32[1,1024,3]{1,2,0:T(4,128)S(1)} copy(s32[1,1024,3]{1,0,2:T(1,128)} %param.10) | data formatting | bytes 24576
  1.4 0.6 %pad_add_fusion.spot_ref = s32[2,1024]{1,0:T(2,128)} fusion(s32[1,1024]{1,0:T(1,128)S(1)} %get-tuple-element.7, s32[1,1024]{1,0:T(1,128)S(1)} %get-tuple-element.6), kind=kLoop, calls=%fused_computation.1 | loop fusion | flops 2048 | bytes 16384 | tf_op jit(solution)/shard_map/stack | solution.py:325
  2.0 40.5 %shard_map.77 = (f32[16,32,128]{2,1,0:T(8,128)}, f32[2,16,128,128]{3,2,1,0:T(8,128)}) custom-call(s32[3]{0:T(128)} %bitcast.17, s32[2,1024]{1,0:T(2,128)} %pad_add_fusion.spot_ref, f32[4,1024]{1,0:T(4,128)} %bitcast.16, f32[16,128,128]{2,1,0:T(8,128)} %courant_hbm.1, f32[2,16,128,128]{3,2,1,0:T(8,128)} %bitcast.13, bf16[6,16,128,128]{3,2,1,0:T(8,128)(2,1)} %bitcast.12), custom_call_target="tpu_custom_call" | custom-call | tf_op jit(solution)/shard_map/pallas_call | solution.py:328
  42.5 1.7 %copy.13 = f32[16,32,128]{2,1,0:T(8,128)} copy(f32[16,32,128]{2,1,0:T(8,128)} %get-tuple-element.10) | data formatting | bytes 524288
  44.1 3.1 %copy.14 = f32[1,2,16,128,128]{4,3,2,1,0:T(8,128)} copy(f32[1,2,16,128,128]{4,3,2,1,0:T(8,128)} %bitcast.14) | data formatting | bytes 4194304
  (1 shorter events, 0.0 us)

commit v2 on v1

--- a/solution.py
+++ b/solution.py
@@ -25,7 +25,7 @@
     init_hbm,
     fwd_hbm,
     grad_ref,
-    final_hbm,
+    final_ref,
     lev,
     courant,
     fwd,
@@ -39,7 +39,6 @@
     recv_sem,
     part_send,
     part_recv,
-    out_sem,
 ):
     slab, size_x, size_y = courant.shape
     rows = size_x // shot_n
@@ -87,11 +86,19 @@
         barrier, has_up.astype(jnp.int32) + has_down.astype(jnp.int32) + (shot_n - 1)
     )
 
+    def owner(i):
+        i = i + 1
+        if shot_n % 2:
+            return lax.rem(shot + i, shot_n)
+        pair = lax.rem(lax.div(shot, 2) + (i // 2 + i % 2) % (shot_n // 2), shot_n // 2)
+        return pair * 2 + lax.rem(shot + i, 2)
+
     def halo_copies(step, strip):
         level = step + 1
-        cut = pl.ds(PAD + strip * rows, rows)
+        begin = pl.multiple_of(owner(strip) * rows, 8)
+        cut = pl.ds(pl.multiple_of(PAD + begin, 8), rows)
         if step == 0:
-            plain = pl.ds(strip * rows, rows)
+            plain = pl.ds(begin, rows)
             low = init_hbm.at[1, pl.ds(0, HALO), plain, :]
             high = init_hbm.at[1, pl.ds(slab - HALO, HALO), plain, :]
         else:
@@ -163,12 +170,12 @@
         weights = jnp.where(gap == offset, jnp.float32(STENCIL_WEIGHTS[offset]), weights)
     band[...] = weights
 
-    n_rec = spot_ref.shape[1]
+    n_rec = spot_ref.shape[2]
 
     @pl.loop(0, slab)
     def _(z):
         row = lax.broadcasted_iota(jnp.int32, (size_x, n_rec), 0) + z * size_x
-        same = row == spot_ref[0:1, :]
+        same = row == (spot_ref[0] - me * slab) * size_x + spot_ref[1]
         hot[pl.ds(pl.multiple_of(z * size_x, size_x), size_x), :] = jnp.where(
             same, 1.0, 0.0
         ).astype(jnp.bfloat16)
@@ -177,7 +184,7 @@
         amount = trace_ref[section : section + 1, :]
         high = amount.astype(jnp.bfloat16).astype(jnp.float32)
         low = amount - high
-        same = lax.broadcasted_iota(jnp.int32, (size_y, n_rec), 0) == spot_ref[1:2, :]
+        same = lax.broadcasted_iota(jnp.int32, (size_y, n_rec), 0) == spot_ref[2]
         columns = jnp.concatenate(
             [jnp.where(same, high, 0.0), jnp.where(same, low, 0.0)], axis=0
         ).astype(jnp.bfloat16)
@@ -222,7 +229,10 @@
         added = added[0][None] if planes == 1 else jnp.stack(added)
         later = lev[level - 1, pl.ds(HALO + z, planes), cut, :]
         new = 2.0 * now - later + courant[here, plain, :] * total + added
-        lev[level + 1, pl.ds(HALO + z, planes), cut, :] = new
+        if step < ITERS - 1:
+            lev[level + 1, pl.ds(HALO + z, planes), cut, :] = new
+        if step >= ITERS - 2:
+            final_ref[step - (ITERS - 2), here, plain, :] = new
         accel = (
             fwd[section + 2, here, plain, :].astype(jnp.float32)
             - 2.0 * fwd[section + 1, here, plain, :].astype(jnp.float32)
@@ -240,27 +250,19 @@
             value = value * (1.0 - jnp.exp(distance * (-1.0 / float(RADIUS * RADIUS))))
         image[here, plain, :] = value
 
-    def part_copy(d, group, first_z, planes):
-        target = lax.rem(shot + d, shot_n)
+    def part_copy(i, group):
+        first_z, planes = groups[group]
         return pltpu.make_async_remote_copy(
             src_ref=image.at[
-                pl.ds(first_z, planes), pl.ds(pl.multiple_of(target * rows, 8), rows), :
+                pl.ds(first_z, planes), pl.ds(pl.multiple_of(owner(i) * rows, 8), rows), :
             ],
-            dst_ref=parts.at[d - 1, pl.ds(first_z, planes), :, :],
-            send_sem=part_send.at[group, d - 1],
-            recv_sem=part_recv.at[group, d - 1],
-            device_id={"shot": target},
+            dst_ref=parts.at[i, pl.ds(first_z, planes), :, :],
+            send_sem=part_send.at[group, i],
+            recv_sem=part_recv.at[group, i],
+            device_id={"shot": owner(i)},
         )
 
     groups = ((HALO, slab - 2 * HALO), (0, HALO), (slab - HALO, HALO))
-
-    def final_copy(index, group):
-        first_z, planes = groups[group]
-        return pltpu.make_async_copy(
-            lev.at[ITERS + index, pl.ds(HALO + first_z, planes), pl.ds(PAD, size_x), :],
-            final_hbm.at[index, pl.ds(first_z, planes)],
-            out_sem.at[index, group],
-        )
 
     for step in range(ITERS):
         last = step == ITERS - 1
@@ -274,44 +276,35 @@
             update(step, z, 1, 0, size_x)
 
         if last:
-            final_copy(1, 0).start()
-            for d in range(1, shot_n):
-                part_copy(d, 0, *groups[0]).start()
-
-        for strip in range(shot_n):
-            wait_halo(step, strip)
-            update(step, 0, HALO, strip * rows, rows)
-            update(step, slab - HALO, HALO, strip * rows, rows)
+            for i in range(shot_n - 1):
+                part_copy(i, 0).start()
+
+        for i in range(shot_n):
+            first = pl.multiple_of(owner(i) * rows, 8)
+            wait_halo(step, i)
+            update(step, 0, HALO, first, rows)
+            update(step, slab - HALO, HALO, first, rows)
             if not last:
-                send_halo(step + 1, strip)
-
-        if step == ITERS - 2:
-            for group in range(3):
-                final_copy(0, group).start()
-
-    for group in (1, 2):
-        final_copy(1, group).start()
-        for d in range(1, shot_n):
-            part_copy(d, group, *groups[group]).start()
-
+                send_halo(step + 1, i)
+            elif i < shot_n - 1:
+                part_copy(i, 1).start()
+                part_copy(i, 2).start()
+
+    mine = pl.ds(pl.multiple_of(shot * rows, 8), rows)
     for group in range(3):
         first_z, planes = groups[group]
-        value = image[
-            first_z : first_z + planes, pl.ds(pl.multiple_of(shot * rows, 8), rows), :
-        ]
-        for d in range(1, shot_n):
-            part_copy(d, group, first_z, planes).wait_recv()
-            value = value + parts[d - 1, first_z : first_z + planes]
+        value = image[first_z : first_z + planes, mine, :]
+        for i in range(shot_n - 1):
+            part_copy(i, group).wait_recv()
+            value = value + parts[i, first_z : first_z + planes]
         grad_ref[first_z : first_z + planes] = value
 
     for step in range(ITERS):
-        for strip in range(shot_n):
-            wait_sent(step, strip)
+        for i in range(shot_n):
+            wait_sent(step, i)
     for group in range(3):
-        for d in range(1, shot_n):
-            part_copy(d, group, *groups[group]).wait_send()
-        final_copy(0, group).wait()
-        final_copy(1, group).wait()
+        for i in range(shot_n - 1):
+            part_copy(i, group).wait_send()
 
 
 def per_device(
@@ -319,20 +312,17 @@
 ):
     slab, size_x, size_y = courant_sq.shape
     n_rec = receivers.shape[1]
-    first_row = lax.axis_index("dom") * slab
-    spots = receivers[0]
-    spot_rows = (spots[:, 0] - first_row) * size_x + spots[:, 1]
-    spot = jnp.stack([spot_rows, spots[:, 2]])
+    spot = jnp.transpose(receivers, (2, 0, 1))
     hbm = pl.BlockSpec(memory_space=pl.ANY)
     vmem = pl.BlockSpec(memory_space=pltpu.VMEM)
     gradient, final = pl.pallas_call(
         functools.partial(kernel, dom_n, shot_n),
         out_shape=(
-            jax.ShapeDtypeStruct((slab, size_x // shot_n, size_y), jnp.float32),
-            jax.ShapeDtypeStruct((2, slab, size_x, size_y), jnp.float32),
+            pltpu.VMEM((slab, size_x // shot_n, size_y), jnp.float32),
+            pltpu.VMEM((2, slab, size_x, size_y), jnp.float32),
         ),
         in_specs=[pl.BlockSpec(memory_space=pltpu.SMEM), vmem, vmem, hbm, hbm, hbm],
-        out_specs=(vmem, hbm),
+        out_specs=(vmem, vmem),
         scratch_shapes=[
             pltpu.VMEM((ITERS + 2, slab + 2 * HALO, size_x + 2 * PAD, size_y), jnp.float32),
             pltpu.VMEM((slab, size_x, size_y), jnp.float32),
@@ -347,7 +337,6 @@
             pltpu.SemaphoreType.DMA((ITERS, 2, shot_n)),
             pltpu.SemaphoreType.DMA((3, shot_n - 1)),
             pltpu.SemaphoreType.DMA((3, shot_n - 1)),
-            pltpu.SemaphoreType.DMA((2, 3)),
         ],
         compiler_params=pltpu.CompilerParams(
             collective_id=0, has_side_effects=True, vmem_limit_bytes=60 * 1024 * 1024

time: 47.6 us -> 43.5 us (0.914)
  local copies, waits for them, and re-layouts: 5.52 us -> 2.02 us
  other arithmetic: 0.62 us -> 0 us
    unnamed x3 -> x2, local copies, waits for them, and re-layouts: 5.52 us -> 2.02 us
    another operation x1 -> x0, other arithmetic: 0.61 us -> none  [per_device(): spot = jnp.stack([spot_rows, spots[:, 2]])]
where the time goes in v2:
time: 43.5 us; the launch traced here: 43.2 us
  Pallas kernels  40.6 us (93%)
  local copies, waits for them, and re-layouts  2.02 us (5%)
  between operations  0.64 us (1%)
    pallas_call x1, Pallas kernels, per_device(): pl.pallas_call(functools.partial(kernel, dom_n, shot_n), out_shape=(pltpu...  40.6 us
    unnamed x2, local copies, waits for them, and re-layouts  2.02 us

profile of v2, /device:TPU:0, one launch (start us, length us, event | category | flops | bytes accessed | tf_op | source)
XLA Modules:
  0.0 43.2 jit_solution(2801443012722363007)
XLA Ops:
  0.6 40.6 %shard_map.77 = (f32[16,32,128]{2,1,0:T(8,128)S(1)}, f32[2,16,128,128]{3,2,1,0:T(8,128)S(1)}) custom-call(s32[3]{0:T(128)} %bitcast.11, s32[3,1,1024]{2,1,0:T(1,128)} %bitcast.10, f32[4,1024]{1,0:T(4,128)} %bitcast.9, f32[16,128,128]{2,1,0:T(8,128)} %courant_hbm.1, f32[2,16,128,128]{3,2,1,0:T(8,128)} %bitcast.8, bf16[6,16,128,128]{3,2,1,0:T(8,128)(2,1)} %bitcast.7), custom_call_target="tpu_custom_call" | custom-call | tf_op jit(solution)/shard_map/pallas_call | solution.py:318
  41.2 0.7 %copy.10 = f32[16,32,128]{2,1,0:T(8,128)} copy(f32[16,32,128]{2,1,0:T(8,128)S(1)} %get-tuple-element.6) | data formatting | bytes 524288
  41.9 1.3 %copy.11 = f32[1,2,16,128,128]{4,3,2,1,0:T(8,128)} copy(f32[1,2,16,128,128]{4,3,2,1,0:T(8,128)S(1)} %bitcast.6) | data formatting | bytes 4194304

commit v3 on v2

--- a/solution.py
+++ b/solution.py
@@ -168,7 +168,10 @@
     weights = jnp.where(gap == 0, jnp.float32(3.0 * STENCIL_WEIGHTS[0]), jnp.float32(0.0))
     for offset in range(1, HALO + 1):
         weights = jnp.where(gap == offset, jnp.float32(STENCIL_WEIGHTS[offset]), weights)
-    band[...] = weights
+    coarse = weights.astype(jnp.bfloat16)
+    band[0:size_y, :] = coarse
+    band[size_y : 2 * size_y, :] = coarse
+    band[2 * size_y :, :] = (weights - coarse.astype(jnp.float32)).astype(jnp.bfloat16)
 
     n_rec = spot_ref.shape[2]
 
@@ -207,11 +210,13 @@
         plain = pl.ds(first, count)
         here = pl.ds(z, planes)
         now = lev[level, pl.ds(HALO + z, planes), cut, :]
+        flat = now.reshape(planes * count, size_y)
+        high = flat.astype(jnp.bfloat16)
+        low = (flat - high.astype(jnp.float32)).astype(jnp.bfloat16)
         total = lax.dot_general(
-            now.reshape(planes * count, size_y),
+            jnp.concatenate([high, low, high], axis=1),
             band[...],
             (((1,), (0,)), ((), ())),
-            precision=lax.Precision.HIGHEST,
             preferred_element_type=jnp.float32,
         ).reshape(planes, count, size_y)
         for offset in range(1, HALO + 1):
@@ -250,8 +255,11 @@
             value = value * (1.0 - jnp.exp(distance * (-1.0 / float(RADIUS * RADIUS))))
         image[here, plain, :] = value
 
+    paired = shot_n == 4
+
     def part_copy(i, group):
         first_z, planes = groups[group]
+        target = owner(2) if paired and i == 0 else owner(i)
         return pltpu.make_async_remote_copy(
             src_ref=image.at[
                 pl.ds(first_z, planes), pl.ds(pl.multiple_of(owner(i) * rows, 8), rows), :
@@ -259,8 +267,17 @@
             dst_ref=parts.at[i, pl.ds(first_z, planes), :, :],
             send_sem=part_send.at[group, i],
             recv_sem=part_recv.at[group, i],
-            device_id={"shot": owner(i)},
-        )
+            device_id={"shot": target},
+        )
+
+    def part_start(i, group):
+        if paired and i == 1:
+            first_z, planes = groups[group]
+            strip = pl.ds(pl.multiple_of(owner(1) * rows, 8), rows)
+            part_copy(0, group).wait_recv()
+            here = pl.ds(first_z, planes)
+            image[here, strip, :] = image[here, strip, :] + parts[0, here]
+        part_copy(i, group).start()
 
     groups = ((HALO, slab - 2 * HALO), (0, HALO), (slab - HALO, HALO))
 
@@ -271,13 +288,14 @@
             for load in loads:
                 load.wait()
 
-        @pl.loop(HALO, slab - HALO)
+        @pl.loop(HALO, slab - HALO, step=HALO)
         def _(z):
-            update(step, z, 1, 0, size_x)
+            for strip in range(shot_n):
+                update(step, z, HALO, strip * rows, rows)
 
         if last:
-            for i in range(shot_n - 1):
-                part_copy(i, 0).start()
+            for i in (0, 2, 1) if paired else range(shot_n - 1):
+                part_start(i, 0)
 
         for i in range(shot_n):
             first = pl.multiple_of(owner(i) * rows, 8)
@@ -287,14 +305,14 @@
             if not last:
                 send_halo(step + 1, i)
             elif i < shot_n - 1:
-                part_copy(i, 1).start()
-                part_copy(i, 2).start()
+                part_start(i, 1)
+                part_start(i, 2)
 
     mine = pl.ds(pl.multiple_of(shot * rows, 8), rows)
     for group in range(3):
         first_z, planes = groups[group]
         value = image[first_z : first_z + planes, mine, :]
-        for i in range(shot_n - 1):
+        for i in (1, 2) if paired else range(shot_n - 1):
             part_copy(i, group).wait_recv()
             value = value + parts[i, first_z : first_z + planes]
         grad_ref[first_z : first_z + planes] = value
@@ -330,7 +348,7 @@
             pltpu.VMEM((slab, size_x, size_y), jnp.float32),
             pltpu.VMEM((slab * size_x, n_rec), jnp.bfloat16),
             pltpu.VMEM((slab * size_x, 2 * size_y), jnp.float32),
-            pltpu.VMEM((size_y, size_y), jnp.float32),
+            pltpu.VMEM((3 * size_y, size_y), jnp.bfloat16),
             pltpu.VMEM((shot_n - 1, slab, size_x // shot_n, size_y), jnp.float32),
             pltpu.SemaphoreType.DMA((4,)),
             pltpu.SemaphoreType.DMA((ITERS, 2, shot_n)),

time: 43.5 us -> 38.8 us (0.89)
  Pallas kernels: 40.6 us -> 35.9 us
    pallas_call x1, Pallas kernels: 40.6 us -> 35.9 us  [per_device(): pl.pallas_call(functools.partial(kernel, dom_n, shot_n), out_shape=(pltpu...]
where the time goes in v3:
time: 38.8 us; the launch traced here: 38.6 us
  Pallas kernels  35.9 us (93%)
  local copies, waits for them, and re-layouts  2.02 us (5%)
  between operations  0.64 us (2%)
    pallas_call x1, Pallas kernels, per_device(): pl.pallas_call(functools.partial(kernel, dom_n, shot_n), out_shape=(pltpu...  35.9 us
    unnamed x2, local copies, waits for them, and re-layouts  2.02 us

profile of v3, /device:TPU:0, one launch (start us, length us, event | category | flops | bytes accessed | tf_op | source)
XLA Modules:
  0.0 38.6 jit_solution(14481337686025030790)
XLA Ops:
  0.6 35.9 %shard_map.77 = (f32[16,32,128]{2,1,0:T(8,128)S(1)}, f32[2,16,128,128]{3,2,1,0:T(8,128)S(1)}) custom-call(s32[3]{0:T(128)} %bitcast.11, s32[3,1,1024]{2,1,0:T(1,128)} %bitcast.10, f32[4,1024]{1,0:T(4,128)} %bitcast.9, f32[16,128,128]{2,1,0:T(8,128)} %courant_hbm.1, f32[2,16,128,128]{3,2,1,0:T(8,128)} %bitcast.8, bf16[6,16,128,128]{3,2,1,0:T(8,128)(2,1)} %bitcast.7), custom_call_target="tpu_custom_call" | custom-call | tf_op jit(solution)/shard_map/pallas_call | solution.py:336
  36.5 0.7 %copy.10 = f32[16,32,128]{2,1,0:T(8,128)} copy(f32[16,32,128]{2,1,0:T(8,128)S(1)} %get-tuple-element.6) | data formatting | bytes 524288
  37.3 1.3 %copy.11 = f32[1,2,16,128,128]{4,3,2,1,0:T(8,128)} copy(f32[1,2,16,128,128]{4,3,2,1,0:T(8,128)S(1)} %bitcast.6) | data formatting | bytes 4194304
